TPU v7x, 32 devices: a whole 2x2x4 slice. The times are simulated.
32 devices in a mesh: er: 2 (over x), ec: 4 (over z), dp: 4 (over y, core).
Axes of the slice: x: 2, y: 2, z: 4, core: 2. Of those that a mesh axis runs over, the one named last changes fastest.
Arguments:
- out_grad: bfloat16 [4, 512, 4096], P('dp', 'er', 'ec'), may hold values from -6 to 6
- route_probs: float32 [4, 512], P('dp', 'er'), may hold values from 0.1 to 1
- expert_ids: int32 [4, 512], P('dp', 'er'), may hold values from 0 to 1, as said below
- slot_ids: int32 [4, 512], P('dp', 'er'), may hold values from 0 to 143, as said below
- gate_pre: bfloat16 [4, 2, 288, 768], P('dp', 'er'), may hold values from -6 to 6
- up_act: bfloat16 [4, 2, 288, 768], P('dp', 'er'), may hold values from -6 to 6
- w_gate: bfloat16 [2, 4096, 768], P('er', 'ec'), may hold values from -0.09375 to 0.09375
- w_up: bfloat16 [2, 4096, 768], P('er', 'ec'), may hold values from -0.09375 to 0.09375
- w_down: bfloat16 [2, 768, 4096], P('er', None, 'ec'), may hold values from -0.21875 to 0.21875
Outputs:
- input_grad: bfloat16 [4, 512, 4096], P('dp', 'er', 'ec')
- down_grad: float32 [2, 768, 4096], P('er', 'dp', 'ec')
Inputs may be any that keep to these rules, and one draw needn't show every extreme that they name: `expert_ids`: within each group of 256 tokens no expert is chosen by more than 144 tokens; in every replica some expert is chosen by exactly 144 tokens of every group of that replica. `slot_ids`: tokens of one group that chose the same expert have distinct slots.
All inputs are finite; a program needn't handle non-finite values.
Results may differ from a plain program's by a relative error of at most 0.015.
Values may be sent and summed in bfloat16 or wider, within the bound.
No kernel may reach another device: no remote copies, remote signals or barrier semaphores. Data moves between devices by JAX's collectives and lax.ppermute only.
A program may use at most 64 MiB of HBM per device.

v0:
```python
import jax
import jax.numpy as jnp
from jax import lax
from jax.sharding import PartitionSpec as P


def swiglu_grads(hid_grad, pre_rows, up_rows):
    pre_float = pre_rows.astype(jnp.float32)
    up_float = up_rows.astype(jnp.float32)
    sigmoid = jax.nn.sigmoid(pre_float)
    gate_grad = (hid_grad * up_float * sigmoid * (1.0 + pre_float * (1.0 - sigmoid))).astype(
        jnp.bfloat16
    )
    up_grad = (hid_grad * pre_float * sigmoid).astype(jnp.bfloat16)
    return (gate_grad, up_grad)


def reduce_weights(hidden, arrived):
    replicas = lax.axis_size("dp")
    summed = lax.psum_scatter(
        lax.dot_general(
            hidden, arrived, (((0,), (0,)), ((), ())), preferred_element_type=jnp.float32
        ),
        "dp",
        scatter_dimension=0,
        tiled=True,
    )
    return summed / replicas


def body(out_grad, route_probs, expert_ids, slot_ids, gate_pre, up_act, w_gate, w_up, w_down):
    tokens = out_grad[0]
    experts = lax.axis_size("er")
    capacity = gate_pre.shape[2] // experts
    slot_count = experts * capacity
    position = expert_ids[0] * capacity + slot_ids[0]
    scaled = (route_probs[0][:, None] * tokens.astype(jnp.float32)).astype(jnp.bfloat16)
    source = (
        jnp.zeros((slot_count,), jnp.int32)
        .at[position]
        .set(jnp.arange(tokens.shape[0], dtype=jnp.int32))
    )
    filled = jnp.zeros((slot_count,), jnp.bool_).at[position].set(True)
    outgoing = jnp.where(filled[:, None], scaled[source], jnp.zeros((), jnp.bfloat16))
    arrived = lax.all_to_all(outgoing, "er", split_axis=0, concat_axis=0, tiled=True)
    pre_rows = gate_pre[0, 0]
    up_rows = up_act[0, 0]
    pre_float = pre_rows.astype(jnp.float32)
    hidden = (pre_float * jax.nn.sigmoid(pre_float) * up_rows.astype(jnp.float32)).astype(
        jnp.bfloat16
    )
    partial_value = lax.dot_general(
        arrived, w_down[0], (((1,), (1,)), ((), ())), preferred_element_type=jnp.float32
    )
    hid_grad = lax.psum(partial_value.astype(jnp.bfloat16), "ec").astype(jnp.float32)
    gate_grad, up_grad = swiglu_grads(hid_grad, pre_rows, up_rows)
    slot_grad = (
        lax.dot_general(
            gate_grad, w_gate[0], (((1,), (1,)), ((), ())), preferred_element_type=jnp.float32
        )
        + lax.dot_general(
            up_grad, w_up[0], (((1,), (1,)), ((), ())), preferred_element_type=jnp.float32
        )
    ).astype(jnp.bfloat16)
    returned = lax.all_to_all(slot_grad, "er", split_axis=0, concat_axis=0, tiled=True)
    down_part = reduce_weights(hidden, arrived)
    input_grad = returned[position]
    return (input_grad[None], down_part[None])


def solution(mesh):
    in_specs = (
        P("dp", "er", "ec"),
        P("dp", "er"),
        P("dp", "er"),
        P("dp", "er"),
        P("dp", "er", None, None),
        P("dp", "er", None, None),
        P("er", "ec", None),
        P("er", "ec", None),
        P("er", None, "ec"),
    )
    out_specs = (P("dp", "er", "ec"), P("er", "dp", "ec"))
    return jax.shard_map(body, mesh=mesh, in_specs=in_specs, out_specs=out_specs, check_vma=False)
```

profile of v0, /device:TPU:0, one launch (start us, length us, event | category | flops | bytes accessed | tf_op | source)
XLA Modules:
  0.0 94.2 jit_solution(13919401980403054712)
XLA Ops:
  8.0 0.0 copy-start
  8.0 0.0 all-reduce.2.cloned.1.call-start
  8.1 0.8 compare_select_fusion
  8.9 1.5 %scatter_custom_fusion = pred[288]{0:T(512)(128)(4,1)S(1)} fusion(s32[256]{0:T(256)S(1)} %bitcast.74, pred[256]{0:T(512)(128)(4,1)S(1)} %broadcast.48, pred[]{:T(512)} %constant.9.clone.1), kind=kCustom, calls=%fused_computation.49 | custom fusion | bytes 289 | tf_op jit(solution)/shard_map/scatter | solution.py:43
  10.4 0.1 broadcast_in_dim.35
  10.5 1.4 %scatter_custom_fusion.1 = s32[288]{0:T(512)S(1)} fusion(s32[256]{0:T(256)S(1)} %bitcast.75, s32[256]{0:T(256)S(1)} %iota.3, s32[]{:T(128)} %constant.2.clone.1), kind=kCustom, calls=%fused_computation.47 | custom fusion | bytes 1156 | tf_op jit(solution)/shard_map/scatter | solution.py:41
  11.9 1.2 %fusion.18 = bf16[256,1024]{1,0:T(8,128)(2,1)S(1)} fusion(bf16[1,256,1024]{2,1,0:T(8,128)(2,1)} %param.9, f32[256]{0:T(256)} %bitcast.77), kind=kLoop, calls=%fused_computation.23 | loop fusion | flops 786432 | bytes 1049600 | tf_op jit(solution)/shard_map/convert_element_type | solution.py:37
  13.1 2.1 %gather_fusion = bf16[288,1024]{1,0:T(8,128)(2,1)S(1)} fusion(bf16[256,1024]{1,0:T(8,128)(2,1)S(1)} %fusion.18, s32[1024]{0:T(1024)S(1)} %pad_clamp_fusion.1), kind=kCustom, calls=%fused_computation | custom fusion | bytes 1180800 | tf_op jit(solution)/shard_map/gather | solution.py:44
  15.2 0.0 copy-start.1
  15.2 0.1 broadcast_select_fusion
  15.3 12.8 %all_to_all.21 = bf16[2,144,1024]{2,1,0:T(8,128)(2,1)S(1)} all-to-all(bf16[2,144,1024]{2,1,0:T(8,128)(2,1)S(1)} %broadcast_select_fusion), channel_id=1, replica_groups=mesh['er'=2,'ec'=4,'dp'=4] {'er'}, dimensions={0} | all-to-all | bytes 1179648 | tf_op jit(solution)/shard_map/all_to_all | solution.py:45
  28.1 0.0 copy-done.1
  28.1 0.0 copy-start.3
  28.1 0.0 copy-start.4
  28.2 1.5 %fusion.15 = bf16[288,768]{1,0:T(8,128)(2,1)} fusion(bf16[288,1024]{1,0:T(8,128)(2,1)S(1)} %bitcast.71, bf16[1,768,1024]{2,1,0:T(8,128)(2,1)S(1)} %copy-done.1), kind=kOutput, calls=%fused_computation.18 | convolution fusion | flops 453206016 | bytes 2605056 | tf_op jit(solution)/shard_map/dot_general | solution.py:52
  29.6 0.0 all-reduce.2.cloned.1.call-update
  29.6 0.0 reduce-scatter.2.cloned.1.call-start
  29.7 0.0 copy-done.3
  29.7 0.0 copy-done.4
  29.7 2.7 %fusion.34 = f32[768,1024]{1,0:T(8,128)} fusion(bf16[288,1024]{1,0:T(8,128)(2,1)S(1)} %bitcast.72, bf16[1,1,288,768]{3,2,1,0:T(8,128)(2,1)S(1)} %copy-done.4, bf16[1,1,288,768]{3,2,1,0:T(8,128)(2,1)S(1)} %copy-done.3), kind=kOutput, calls=%fused_computation.39 | convolution fusion | flops 454754304 | bytes 4620288 | tf_op jit(solution)/shard_map/dot_general | solution.py:21
  32.4 0.0 reduce-scatter.2.cloned.1.call-update
  32.5 35.2 %all-reduce.2.cloned.1.call-done = bf16[288,768]{1,0:T(8,128)(2,1)} async-done(((bf16[288,768]{1,0:T(8,128)(2,1)}), bf16[288,768]{1,0:T(8,128)(2,1)}) %all-reduce.2.cloned.1.call-update) | async-done | bytes 442384 | tf_op jit(solution)/shard_map/psum | solution.py:55
  67.7 0.0 copy-done
  67.7 0.0 copy-start.2
  67.7 0.0 copy-start.5
  67.7 1.8 %fusion = f32[288,1024]{1,0:T(8,128)S(1)} fusion(bf16[1,1024,768]{2,1,0:T(8,128)(2,1)S(1)} %copy-done, bf16[1,1,288,768]{3,2,1,0:T(8,128)(2,1)S(1)} %copy-done.3, bf16[288,768]{1,0:T(8,128)(2,1)} %all-reduce.2.cloned.1.call-done), kind=kOutput, calls=%fused_computation.4 | convolution fusion | flops 454754304 | bytes 3637248 | tf_op jit(solution)/shard_map/dot_general | solution.py:61
  69.6 0.0 copy-done.2
  69.6 0.0 copy-done.5
  69.6 1.7 %fusion.12 = bf16[288,1024]{1,0:T(8,128)(2,1)} fusion(f32[288,1024]{1,0:T(8,128)S(1)} %fusion, bf16[1,1024,768]{2,1,0:T(8,128)(2,1)S(1)} %copy-done.2, bf16[288,768]{1,0:T(8,128)(2,1)S(1)} %copy-done.5, bf16[1,1,288,768]{3,2,1,0:T(8,128)(2,1)S(1)} %copy-done.4, bf16[1,1,288,768]{3,2,1,0:T(8,128)(2,1)S(1)} %copy-done.3), kind=kOutput, calls=%fused_computation.17 | convolution fusion | flops 456450048 | bytes 4669440 | tf_op jit(solution)/shard_map/dot_general | solution.py:58
  71.2 3.5 %all-to-all-start.1 = ((bf16[2,144,1024]{2,1,0:T(8,128)(2,1)}), bf16[2,144,1024]{2,1,0:T(8,128)(2,1)S(1)}, u32[]{:S(2)}, u32[]{:S(2)}) async-start(bf16[2,144,1024]{2,1,0:T(8,128)(2,1)} %bitcast.11), calls=%async_computation.1 | async-start | bytes 1179648 | tf_op jit(solution)/shard_map/all_to_all | solution.py:65
  74.8 8.0 %all-to-all-done.1 = bf16[2,144,1024]{2,1,0:T(8,128)(2,1)S(1)} async-done(((bf16[2,144,1024]{2,1,0:T(8,128)(2,1)}), bf16[2,144,1024]{2,1,0:T(8,128)(2,1)S(1)}, u32[]{:S(2)}, u32[]{:S(2)}) %all-to-all-start.1) | async-done | bytes 589856 | tf_op jit(solution)/shard_map/all_to_all | solution.py:65
  82.7 2.0 %gather_fusion.1 = bf16[256,1024]{1,0:T(8,128)(2,1)} fusion(bf16[288,1024]{1,0:T(8,128)(2,1)S(1)} %bitcast.69, s32[1024]{0:T(1024)S(1)} %pad_clamp_fusion), kind=kCustom, calls=%fused_computation.1 | custom fusion | bytes 1049600 | tf_op jit(solution)/shard_map/gather | solution.py:67
  84.7 0.0 reduce-scatter.2.cloned.1.call-done
  84.7 2.1 %multiply_bitcast_fusion = f32[1,192,1024]{2,1,0:T(8,128)} fusion(f32[192,1024]{1,0:T(8,128)} %reduce-scatter.2.cloned.1.call-done), kind=kLoop, calls=%fused_computation.37 | loop fusion | flops 196608 | bytes 1572864 | tf_op jit(solution)/shard_map/broadcast_in_dim | solution.py:68
  (5 shorter events, 0.0 us)
Async XLA Ops:
  8.0 59.7 %copy-start = (bf16[1,1024,768]{2,1,0:T(8,128)(2,1)S(1)}, bf16[1,1024,768]{2,1,0:T(8,128)(2,1)}, u32[]{:S(2)}) copy-start(bf16[1,1024,768]{2,1,0:T(8,128)(2,1)} %param.16) | copy-start | bytes 4718596
  8.0 59.7 %all-reduce.2.cloned.1.call-start = ((), (), s32[]{:S(2)}) async-start(), calls=%async_computation.3 | async-start | bytes 884736 | tf_op jit(solution)/shard_map/psum | solution.py:55
  15.2 13.0 %copy-start.1 = (bf16[1,768,1024]{2,1,0:T(8,128)(2,1)S(1)}, bf16[1,768,1024]{2,1,0:T(8,128)(2,1)}, u32[]{:S(2)}) copy-start(bf16[1,768,1024]{2,1,0:T(8,128)(2,1)} %param.17) | copy-start | bytes 4718596
  28.1 1.5 %copy-start.3 = (bf16[1,1,288,768]{3,2,1,0:T(8,128)(2,1)S(1)}, bf16[1,1,288,768]{3,2,1,0:T(8,128)(2,1)}, u32[]{:S(2)}) copy-start(bf16[1,1,288,768]{3,2,1,0:T(8,128)(2,1)} %param.13) | copy-start | bytes 1327108
  28.1 1.5 %copy-start.4 = (bf16[1,1,288,768]{3,2,1,0:T(8,128)(2,1)S(1)}, bf16[1,1,288,768]{3,2,1,0:T(8,128)(2,1)}, u32[]{:S(2)}) copy-start(bf16[1,1,288,768]{3,2,1,0:T(8,128)(2,1)} %param.14) | copy-start | bytes 1327108
  29.6 55.0 %reduce-scatter.2.cloned.1.call-start = ((), (), s32[]{:S(2)}) async-start(), calls=%async_computation.4 | async-start | bytes 3932160 | tf_op jit(solution)/shard_map/reduce_scatter | solution.py:20
  67.7 1.8 %copy-start.2 = (bf16[1,1024,768]{2,1,0:T(8,128)(2,1)S(1)}, bf16[1,1024,768]{2,1,0:T(8,128)(2,1)}, u32[]{:S(2)}) copy-start(bf16[1,1024,768]{2,1,0:T(8,128)(2,1)} %param.15) | copy-start | bytes 4718596
  67.7 1.9 %copy-start.5 = (bf16[288,768]{1,0:T(8,128)(2,1)S(1)}, bf16[288,768]{1,0:T(8,128)(2,1)}, u32[]{:S(2)}) copy-start(bf16[288,768]{1,0:T(8,128)(2,1)} %all-reduce.2.cloned.1.call-done) | copy-start | bytes 1327108
  71.2 11.5 %all-to-all-start.1 = ((bf16[2,144,1024]{2,1,0:T(8,128)(2,1)}), bf16[2,144,1024]{2,1,0:T(8,128)(2,1)S(1)}, u32[]{:S(2)}, u32[]{:S(2)}) async-start(bf16[2,144,1024]{2,1,0:T(8,128)(2,1)} %bitcast.11), calls=%async_computation.1 | async-start | bytes 1179648 | tf_op jit(solution)/shard_map/all_to_all | solution.py:65
Sparse Core Ops, SparseCore 0:
  29.8 37.9 all-reduce.1
Sparse Core Ops, SparseCore 1:
  32.6 38.2 reduce-scatter.1
where the time goes:
time: 94.6 us; the launch traced here: 94.2 us
  waiting for transfers between devices  43.2 us (46%)
  between operations  15.6 us (16%)
  blocking collectives  12.8 us (14%)
  matrix products  7.69 us (8%)
  local copies, waits for them, and re-layouts  7.04 us (7%)
  other arithmetic  4.23 us (4%)
  starting transfers between devices  3.58 us (4%)
    psum x1, waiting for transfers between devices, body(): lax.psum(partial_value.astype(jnp.bfloat16), 'ec').astype(jnp.float32)  35.2 us
    all_to_all x1, blocking collectives, body(): lax.all_to_all(outgoing, 'er', split_axis=0, concat_axis=0, tiled=True)  12.8 us
    all_to_all x1, waiting for transfers between devices, body(): lax.all_to_all(slot_grad, 'er', split_axis=0, concat_axis=0, tiled=True)  7.97 us
    all_to_all x1, starting transfers between devices, body(): lax.all_to_all(slot_grad, 'er', split_axis=0, concat_axis=0, tiled=True)  3.5 us
    dot_general x1, matrix products, reduce_weights(): lax.dot_general(hidden, arrived, (((0,), (0,)), ((), ())), preferred_elem...  2.75 us
    broadcast_in_dim x1, other arithmetic, body(): return (input_grad[None], down_part[None])  2.1 us
    gather x1, local copies, waits for them, and re-layouts, body(): scaled[source]  2.07 us
    gather x1, local copies, waits for them, and re-layouts, body(): input_grad = returned[position]  1.96 us
  transfers between devices with their start and end apart: 3, of which 2 were waited for; matrix products, arithmetic and copies ran while one was open for 9% of the time, Pallas kernels for 0%

commit v1 on v0

--- a/solution.py
+++ b/solution.py
@@ -52,7 +52,9 @@
     partial_value = lax.dot_general(
         arrived, w_down[0], (((1,), (1,)), ((), ())), preferred_element_type=jnp.float32
     )
-    hid_grad = lax.psum(partial_value.astype(jnp.bfloat16), "ec").astype(jnp.float32)
+    hid_grad = jnp.sum(lax.all_gather(partial_value.astype(jnp.bfloat16), "ec"), axis=0).astype(
+        jnp.float32
+    )
     gate_grad, up_grad = swiglu_grads(hid_grad, pre_rows, up_rows)
     slot_grad = (
         lax.dot_general(

time: 94.6 us -> 99.5 us (1.052)
  waiting for transfers between devices: 43.2 us -> 46.6 us
  other arithmetic: 4.23 us -> 6.18 us
  matrix products: 7.69 us -> 6.57 us
    all_gather x0 -> x1, waiting for transfers between devices: none -> 38 us  [body(): lax.all_gather(partial_value.astype(jnp.bfloat16), 'ec')]
    psum x1 -> x0, waiting for transfers between devices: 35.2 us -> none  [body(): lax.psum(partial_value.astype(jnp.bfloat16), 'ec').astype(jnp.float32)]
    reduce_sum x0 -> x1, other arithmetic: none -> 1.94 us  [body(): jnp.sum(lax.all_gather(partial_value.astype(jnp.bfloat16), 'ec'), axis=0)]
    dot_general x1, matrix products: 1.84 us -> 0.67 us  [body(): lax.dot_general(up_grad, w_up[0], (((1,), (1,)), ((), ())), preferred_ele...]
where the time goes in v1:
time: 99.5 us; the launch traced here: 99.2 us
  waiting for transfers between devices  46.6 us (47%)
  between operations  15.6 us (16%)
  blocking collectives  12.8 us (13%)
  local copies, waits for them, and re-layouts  7.75 us (8%)
  matrix products  6.57 us (7%)
  other arithmetic  6.18 us (6%)
  starting transfers between devices  3.58 us (4%)
    all_gather x1, waiting for transfers between devices, body(): lax.all_gather(partial_value.astype(jnp.bfloat16), 'ec')  38 us
    all_to_all x1, blocking collectives, body(): lax.all_to_all(outgoing, 'er', split_axis=0, concat_axis=0, tiled=True)  12.8 us
    all_to_all x1, waiting for transfers between devices, body(): lax.all_to_all(slot_grad, 'er', split_axis=0, concat_axis=0, tiled=True)  8.58 us
    all_to_all x1, starting transfers between devices, body(): lax.all_to_all(slot_grad, 'er', split_axis=0, concat_axis=0, tiled=True)  3.5 us
    dot_general x1, matrix products, reduce_weights(): lax.dot_general(hidden, arrived, (((0,), (0,)), ((), ())), preferred_elem...  2.76 us
    broadcast_in_dim x1, other arithmetic, body(): return (input_grad[None], down_part[None])  2.1 us
    gather x1, local copies, waits for them, and re-layouts, body(): scaled[source]  2.07 us
  transfers between devices with their start and end apart: 3, of which 2 were waited for; matrix products, arithmetic and copies ran while one was open for 9% of the time, Pallas kernels for 0%

profile of v1, /device:TPU:0, one launch (start us, length us, event | category | flops | bytes accessed | tf_op | source)
XLA Modules:
  0.0 99.2 jit_solution(13886294739210671548)
XLA Ops:
  8.0 0.0 copy-start
  8.0 0.0 all-gather.3.cloned.1.call-start
  8.1 0.8 compare_select_fusion
  8.9 1.5 %scatter_custom_fusion = pred[288]{0:T(512)(128)(4,1)S(1)} fusion(s32[256]{0:T(256)S(1)} %bitcast.59, pred[256]{0:T(512)(128)(4,1)S(1)} %broadcast.51, pred[]{:T(512)} %constant.9.clone.1), kind=kCustom, calls=%fused_computation.44 | custom fusion | bytes 289 | tf_op jit(solution)/shard_map/scatter | solution.py:43
  10.4 0.1 broadcast_in_dim.35
  10.5 1.4 %scatter_custom_fusion.1 = s32[288]{0:T(512)S(1)} fusion(s32[256]{0:T(256)S(1)} %bitcast.60, s32[256]{0:T(256)S(1)} %iota.3, s32[]{:T(128)} %constant.2.clone.1), kind=kCustom, calls=%fused_computation.42 | custom fusion | bytes 1156 | tf_op jit(solution)/shard_map/scatter | solution.py:41
  11.9 1.2 %fusion.15 = bf16[256,1024]{1,0:T(8,128)(2,1)S(1)} fusion(bf16[1,256,1024]{2,1,0:T(8,128)(2,1)} %param.9, f32[256]{0:T(256)} %bitcast.62), kind=kLoop, calls=%fused_computation.20 | loop fusion | flops 786432 | bytes 1049600 | tf_op jit(solution)/shard_map/convert_element_type | solution.py:37
  13.1 2.1 %gather_fusion = bf16[288,1024]{1,0:T(8,128)(2,1)S(1)} fusion(bf16[256,1024]{1,0:T(8,128)(2,1)S(1)} %fusion.15, s32[1024]{0:T(1024)S(1)} %pad_clamp_fusion.1), kind=kCustom, calls=%fused_computation | custom fusion | bytes 1180800 | tf_op jit(solution)/shard_map/gather | solution.py:44
  15.2 0.0 copy-start.1
  15.2 0.1 broadcast_select_fusion
  15.3 12.8 %all_to_all.21 = bf16[2,144,1024]{2,1,0:T(8,128)(2,1)S(1)} all-to-all(bf16[2,144,1024]{2,1,0:T(8,128)(2,1)S(1)} %broadcast_select_fusion), channel_id=1, replica_groups=mesh['er'=2,'ec'=4,'dp'=4] {'er'}, dimensions={0} | all-to-all | bytes 1179648 | tf_op jit(solution)/shard_map/all_to_all | solution.py:45
  28.1 0.0 copy-done.1
  28.1 0.0 copy-start.3
  28.1 0.0 copy-start.4
  28.2 1.5 %fusion.12 = bf16[288,768]{1,0:T(8,128)(2,1)} fusion(bf16[288,1024]{1,0:T(8,128)(2,1)S(1)} %bitcast.56, bf16[1,768,1024]{2,1,0:T(8,128)(2,1)S(1)} %copy-done.1), kind=kOutput, calls=%fused_computation.16 | convolution fusion | flops 453206016 | bytes 2605056 | tf_op jit(solution)/shard_map/dot_general | solution.py:52
  29.6 0.0 all-gather.3.cloned.1.call-update
  29.6 0.0 reduce-scatter.2.cloned.1.call-start
  29.7 0.0 copy-done.3
  29.7 0.0 copy-done.4
  29.7 2.8 %fusion.26 = f32[768,1024]{1,0:T(8,128)} fusion(bf16[288,1024]{1,0:T(8,128)(2,1)S(1)} %bitcast.57, bf16[1,1,288,768]{3,2,1,0:T(8,128)(2,1)S(1)} %copy-done.4, bf16[1,1,288,768]{3,2,1,0:T(8,128)(2,1)S(1)} %copy-done.3), kind=kOutput, calls=%fused_computation.33 | convolution fusion | flops 454754304 | bytes 4620288 | tf_op jit(solution)/shard_map/dot_general | solution.py:21
  32.5 0.0 reduce-scatter.2.cloned.1.call-update
  32.5 38.0 %all-gather.3.cloned.1.call-done = bf16[1152,768]{1,0:T(8,128)(2,1)} async-done(((bf16[288,768]{1,0:T(8,128)(2,1)}), bf16[1152,768]{1,0:T(8,128)(2,1)}) %all-gather.3.cloned.1.call-update) | async-done | bytes 1769488 | tf_op jit(solution)/shard_map/all_gather | solution.py:55
  70.5 1.9 %reduce_sum.12 = bf16[288,768]{1,0:T(8,128)(2,1)S(1)} reduce(bf16[4,288,768]{2,1,0:T(8,128)(2,1)} %bitcast.55, bf16[]{:T(256)} %constant.6.clone.1), dimensions={0}, to_apply=%region_2.3 | reduce | flops 663552 | bytes 2211842 | tf_op jit(solution)/shard_map/reduce_sum | solution.py:55
  72.5 0.0 copy-done
  72.5 0.0 copy-start.2
  72.5 0.7 fusion
  73.2 0.7 copy-done.2
  73.9 1.7 %fusion.9 = bf16[288,1024]{1,0:T(8,128)(2,1)} fusion(f32[288,1024]{1,0:T(8,128)S(1)} %fusion, bf16[1,1024,768]{2,1,0:T(8,128)(2,1)S(1)} %copy-done.2, bf16[1,1,288,768]{3,2,1,0:T(8,128)(2,1)S(1)} %copy-done.4, bf16[1,1,288,768]{3,2,1,0:T(8,128)(2,1)S(1)} %copy-done.3, bf16[288,768]{1,0:T(8,128)(2,1)S(1)} %reduce_sum.12), kind=kOutput, calls=%fused_computation.15 | convolution fusion | flops 456450048 | bytes 4669440 | tf_op jit(solution)/shard_map/dot_general | solution.py:60
  75.6 3.5 %all-to-all-start.1 = ((bf16[2,144,1024]{2,1,0:T(8,128)(2,1)}), bf16[2,144,1024]{2,1,0:T(8,128)(2,1)S(1)}, u32[]{:S(2)}, u32[]{:S(2)}) async-start(bf16[2,144,1024]{2,1,0:T(8,128)(2,1)} %bitcast.14), calls=%async_computation.1 | async-start | bytes 1179648 | tf_op jit(solution)/shard_map/all_to_all | solution.py:67
  79.1 8.6 %all-to-all-done.1 = bf16[2,144,1024]{2,1,0:T(8,128)(2,1)S(1)} async-done(((bf16[2,144,1024]{2,1,0:T(8,128)(2,1)}), bf16[2,144,1024]{2,1,0:T(8,128)(2,1)S(1)}, u32[]{:S(2)}, u32[]{:S(2)}) %all-to-all-start.1) | async-done | bytes 589856 | tf_op jit(solution)/shard_map/all_to_all | solution.py:67
  87.7 2.0 %gather_fusion.1 = bf16[256,1024]{1,0:T(8,128)(2,1)} fusion(bf16[288,1024]{1,0:T(8,128)(2,1)S(1)} %bitcast.53, s32[1024]{0:T(1024)S(1)} %pad_clamp_fusion), kind=kCustom, calls=%fused_computation.1 | custom fusion | bytes 1049600 | tf_op jit(solution)/shard_map/gather | solution.py:69
  89.6 0.0 reduce-scatter.2.cloned.1.call-done
  89.6 2.1 %multiply_bitcast_fusion = f32[1,192,1024]{2,1,0:T(8,128)} fusion(f32[192,1024]{1,0:T(8,128)} %reduce-scatter.2.cloned.1.call-done), kind=kLoop, calls=%fused_computation.31 | loop fusion | flops 196608 | bytes 1572864 | tf_op jit(solution)/shard_map/broadcast_in_dim | solution.py:70
  (5 shorter events, 0.0 us)
Async XLA Ops:
  8.0 64.5 %copy-start = (bf16[1,1024,768]{2,1,0:T(8,128)(2,1)S(1)}, bf16[1,1024,768]{2,1,0:T(8,128)(2,1)}, u32[]{:S(2)}) copy-start(bf16[1,1024,768]{2,1,0:T(8,128)(2,1)} %param.16) | copy-start | bytes 4718596
  8.0 62.5 %all-gather.3.cloned.1.call-start = ((), (), s32[]{:S(2)}) async-start(), calls=%async_computation.4 | async-start | bytes 2211840 | tf_op jit(solution)/shard_map/all_gather | solution.py:55
  15.2 13.0 %copy-start.1 = (bf16[1,768,1024]{2,1,0:T(8,128)(2,1)S(1)}, bf16[1,768,1024]{2,1,0:T(8,128)(2,1)}, u32[]{:S(2)}) copy-start(bf16[1,768,1024]{2,1,0:T(8,128)(2,1)} %param.17) | copy-start | bytes 4718596
  28.1 1.5 %copy-start.3 = (bf16[1,1,288,768]{3,2,1,0:T(8,128)(2,1)S(1)}, bf16[1,1,288,768]{3,2,1,0:T(8,128)(2,1)}, u32[]{:S(2)}) copy-start(bf16[1,1,288,768]{3,2,1,0:T(8,128)(2,1)} %param.13) | copy-start | bytes 1327108
  28.1 1.5 %copy-start.4 = (bf16[1,1,288,768]{3,2,1,0:T(8,128)(2,1)S(1)}, bf16[1,1,288,768]{3,2,1,0:T(8,128)(2,1)}, u32[]{:S(2)}) copy-start(bf16[1,1,288,768]{3,2,1,0:T(8,128)(2,1)} %param.14) | copy-start | bytes 1327108
  29.6 60.0 %reduce-scatter.2.cloned.1.call-start = ((), (), s32[]{:S(2)}) async-start(), calls=%async_computation.3 | async-start | bytes 3932160 | tf_op jit(solution)/shard_map/reduce_scatter | solution.py:20
  72.5 1.4 %copy-start.2 = (bf16[1,1024,768]{2,1,0:T(8,128)(2,1)S(1)}, bf16[1,1024,768]{2,1,0:T(8,128)(2,1)}, u32[]{:S(2)}) copy-start(bf16[1,1024,768]{2,1,0:T(8,128)(2,1)} %param.15) | copy-start | bytes 4718596
  75.6 12.1 %all-to-all-start.1 = ((bf16[2,144,1024]{2,1,0:T(8,128)(2,1)}), bf16[2,144,1024]{2,1,0:T(8,128)(2,1)S(1)}, u32[]{:S(2)}, u32[]{:S(2)}) async-start(bf16[2,144,1024]{2,1,0:T(8,128)(2,1)} %bitcast.14), calls=%async_computation.1 | async-start | bytes 1179648 | tf_op jit(solution)/shard_map/all_to_all | solution.py:67
Sparse Core Ops, SparseCore 0:
  29.8 40.7 all-gather.2
Sparse Core Ops, SparseCore 1:
  32.6 38.2 reduce-scatter.1
